TPU v7x, 32 devices: a whole 2x2x4 slice. The times are simulated.
32 devices in a mesh: depth: 8 (over z, x), rows: 4 (over y, core).
Axes of the slice: x: 2, y: 2, z: 4, core: 2. Of those that a mesh axis runs over, the one named last changes fastest.
Arguments:
- density: float32 [128, 64, 1024], P('depth', 'rows'), may hold values from 0 to 1
- bin_of_level: int32 [16], replicated, may hold values from 0 to 7
- absorb_bins: float32 [8], replicated, may hold values from 0.00234375 to 0.0625
- emit_bins: float32 [8], replicated, may hold values from 0.2 to 3
- occupancy: int32 [8, 4, 8], P('depth', 'rows'), may hold values 0 or 1
- col_offsets: int32 [1024], replicated, may hold values from 2 to 6
- row_offsets: int32 [64], P('rows'), may hold values from 2 to 6
Outputs:
- front_transmittance: float32 [8, 64, 1024], P('depth', 'rows')
- final_image: float32 [2, 64, 1024], P(None, 'rows')
All inputs are finite; a program needn't handle non-finite values. No bound on the sum of `occupancy` on one device may be relied on, other than what follows from the above.
Results may differ from a plain program's by a relative error of at most 0.0002.
Values sent between devices are 32-bit elements; how exact they have to be, the bound alone decides.
A program may use at most 64 MiB of HBM per device.

v0:
```python
import jax
import jax.numpy as jnp
from jax import lax
from jax.sharding import PartitionSpec as P


def from_behind(block, axis, distance):
    devices = range(lax.axis_size(axis))
    route = [(i - distance, i) for i in devices if i - distance in devices]
    return lax.ppermute(block, axis, route)


def resample_columns(mixed, col_offsets):
    fraction = col_offsets.astype(jnp.float32) / 8.0
    pad_shape = mixed.shape[:-1] + (1,)
    right_side = jnp.concatenate([mixed[..., 1:], jnp.zeros(pad_shape, jnp.float32)], -1)
    return (1.0 - fraction) * mixed + fraction * right_side


def tables(bin_of_level, absorb_bins, emit_bins):
    count_bins = absorb_bins.shape[0]
    onehot = (bin_of_level[:, None] == jnp.arange(count_bins, dtype=jnp.int32)[None, :]).astype(
        jnp.float32
    )
    return (jnp.sum(onehot * absorb_bins[None, :], 1), jnp.sum(onehot * emit_bins[None, :], 1))


def classify(sampled, absorb_level, emit_level):
    levels = absorb_level.shape[0]
    scaled = sampled * float(levels - 1)
    absorption = jnp.zeros(sampled.shape, jnp.float32)
    emission = jnp.zeros(sampled.shape, jnp.float32)
    for knot_index in range(levels):
        weight = jnp.maximum(0.0, 1.0 - jnp.abs(scaled - float(knot_index)))
        absorption = absorption + weight * absorb_level[knot_index]
        emission = emission + weight * emit_level[knot_index]
    return (absorption, emission)


def composite(absorption, emission):
    inclusive = jnp.cumsum(absorption, 0)
    exclusive = inclusive - absorption
    light = jnp.sum(jnp.exp(-exclusive) * (1.0 - jnp.exp(-absorption)) * emission, 0)
    return (light, inclusive[-1])


def on_device(density, bin_of_level, absorb_bins, emit_bins, occupancy, col_offsets, row_offsets):
    following = from_behind(density[:1], "depth", -1)
    extended = jnp.concatenate([density, following], 0)
    mid_depth = 0.5 * (extended[:-1] + extended[1:])
    row_below = from_behind(mid_depth[:, :1], "rows", -1)
    next_rows = jnp.concatenate([mid_depth[:, 1:], row_below], 1)
    frac_row = (row_offsets.astype(jnp.float32) / 8.0)[None, :, None]
    mixed = (1.0 - frac_row) * mid_depth + frac_row * next_rows
    sampled = resample_columns(mixed, col_offsets)
    absorb_level, emit_level = tables(bin_of_level, absorb_bins, emit_bins)
    occupied = occupancy[0, 0]
    absorption, emission = classify(sampled, absorb_level, emit_level)
    brick_mask = jnp.repeat(occupied.astype(jnp.float32), 128)
    absorption = absorption * brick_mask[None, None, :]
    light, depth_sum = composite(absorption, emission)
    position = lax.axis_index("depth")
    pieces = lax.all_gather(depth_sum[None], "depth", axis=0, tiled=True)
    shard_ids = jnp.arange(pieces.shape[0], dtype=jnp.int32)
    in_front = (shard_ids < position)[:, None, None]
    front_depth = jnp.sum(jnp.where(in_front, pieces, 0.0), 0)
    total_depth = jnp.sum(pieces, 0)
    front = jnp.exp(-front_depth)
    radiance = lax.psum(front * light, "depth")
    final_image = jnp.stack([radiance, jnp.exp(-total_depth)])
    return (front[None], final_image)


def solution(mesh):
    placed = (P("depth", "rows", None), P(), P(), P(), P("depth", "rows", None), P(), P("rows"))
    return jax.shard_map(
        on_device,
        mesh=mesh,
        in_specs=placed,
        out_specs=(P("depth", "rows", None), P(None, "rows", None)),
        check_vma=False,
    )
```

profile of v0, /device:TPU:0, one launch (start us, length us, event | category | flops | bytes accessed | tf_op | source)
XLA Modules:
  0.0 160.8 jit_solution(6802575559535258758)
XLA Ops:
  7.2 0.0 all-reduce.3.cloned.1.call-start
  7.2 0.8 slice.114
  8.1 0.0 copy-start.4
  8.1 1.4 collective-permute-start
  9.5 0.0 copy-done.2
  9.5 0.0 copy-done.3
  9.5 0.0 copy-done.4
  9.5 0.1 select_reduce_fusion.1
  9.6 0.0 copy-start.1
  9.6 0.7 fusion.59
  10.4 0.0 copy-done.5
  10.4 0.0 copy-done.1
  10.4 0.0 copy-start.6
  10.4 0.6 copy-done.6
  11.1 0.1 broadcast_bitcast_fusion
  11.1 0.7 fusion.58
  11.8 3.5 %collective-permute-done = f32[1,16,1024]{2,1,0:T(8,128)S(1)} collective-permute-done((f32[1,16,1024]{2,1,0:T(8,128)S(1)}, f32[1,16,1024]{2,1,0:T(8,128)S(1)}, u32[]{:S(2)}, u32[]{:S(2)}) %collective-permute-start) | collective-permute-done | bytes 65568 | tf_op jit(solution)/shard_map/ppermute | solution.py:10
  15.3 1.7 %fusion.3 = f32[16,16,1024]{2,1,0:T(8,128)S(1)} fusion(f32[16,16,1024]{2,1,0:T(8,128)} %param.7, f32[1,16,1024]{2,1,0:T(8,128)S(1)} %collective-permute-done), kind=kLoop, calls=%fused_computation.24 | loop fusion | flops 786432 | bytes 2162688 | tf_op jit(solution)/shard_map/mul | solution.py:50
  17.1 1.3 collective-permute-start.1
  18.4 0.0 copy-start
  18.4 0.1 slice.152
  18.6 1.7 %collective-permute-done.1 = f32[16,1,1024]{2,1,0:T(1,128)S(1)} collective-permute-done((f32[16,1,1024]{2,1,0:T(1,128)S(1)}, f32[16,1,1024]{2,1,0:T(1,128)S(1)}, u32[]{:S(2)}, u32[]{:S(2)}) %collective-permute-start.1) | collective-permute-done | bytes 65568 | tf_op jit(solution)/shard_map/ppermute | solution.py:10
  20.3 0.0 copy-done
  20.3 0.3 fusion.1
  20.6 0.3 slice.154
  21.0 28.9 %multiply_reduce_fusion = (f32[16,1024]{1,0:T(8,128)S(1)}, f32[16,16,1024]{2,1,0:T(8,128)S(1)}) fusion(f32[]{:T(128)} %bitcast.34, f32[]{:T(128)} %bitcast.33, f32[]{:T(128)} %bitcast.32, f32[]{:T(128)} %bitcast.31, f32[]{:T(128)} %bitcast.30, f32[]{:T(128)} %bitcast.29, f32[]{:T(128)} %bitcast.28, f32[]{:T(128)} %bitcast.27, f32[]{:T(128)} %bitcast.26, ...), kind=kOutput, calls=%fused_computation.4 | output fusion | flops 65781760 | bytes 3222656 | tf_op jit(solution)/shard_map/jit(cumsum)/reduce_window_sum | solution.py:41
  49.8 32.2 %all_gather.3 = f32[8,16,1024]{2,1,0:T(8,128)S(1)} all-gather(f32[1,16,1024]{2,1,0:T(8,128)S(1)} %slice.155), channel_id=1, replica_groups=mesh['depth'=8,'rows'=4] {'depth'}, dimensions={0}, use_global_device_ids=true | all-gather | bytes 589824 | tf_op jit(solution)/shard_map/all_gather | solution.py:63
  82.0 0.1 fusion.57
  82.1 0.7 multiply_bitcast_fusion
  82.8 0.0 all-reduce.3.cloned.1.call-update
  82.8 69.7 %all-reduce.3.cloned.1.call-done = f32[1,16,1024]{2,1,0:T(8,128)} async-done(((f32[1,16,1024]{2,1,0:T(8,128)}), f32[1,16,1024]{2,1,0:T(8,128)}) %all-reduce.3.cloned.1.call-update) | async-done | bytes 65552 | tf_op jit(solution)/shard_map/psum | solution.py:69
  152.5 1.5 pad_maximum_fusion.1
  (10 shorter events, 0.1 us)
Async XLA Ops:
  7.2 145.3 %all-reduce.3.cloned.1.call-start = ((), (), s32[]{:S(2)}) async-start(), calls=%async_computation | async-start | bytes 131072 | tf_op jit(solution)/shard_map/psum | solution.py:69
  8.1 1.5 copy-start.2
  8.1 1.5 copy-start.3
  8.1 1.5 copy-start.4
  8.1 7.2 %collective-permute-start = (f32[1,16,1024]{2,1,0:T(8,128)S(1)}, f32[1,16,1024]{2,1,0:T(8,128)S(1)}, u32[]{:S(2)}, u32[]{:S(2)}) collective-permute-start(f32[1,16,1024]{2,1,0:T(8,128)S(1)} %slice.114), channel_id=1, source_target_pairs={{4,0},{8,4},{12,8},{16,12},{20,16},{24,20},{28,24},{5,1},{9,5},{13... | collective-permute-start | bytes 196616 | tf_op jit(solution)/shard_map/ppermute | solution.py:10
  9.6 0.7 copy-start.5
  9.6 0.8 copy-start.1
  10.4 0.7 copy-start.6
  17.1 3.1 %collective-permute-start.1 = (f32[16,1,1024]{2,1,0:T(1,128)S(1)}, f32[16,1,1024]{2,1,0:T(1,128)S(1)}, u32[]{:S(2)}, u32[]{:S(2)}) collective-permute-start(f32[16,1,1024]{2,1,0:T(1,128)S(1)} %slice.153), channel_id=1, source_target_pairs={{1,0},{2,1},{3,2},{5,4},{6,5},{7,6},{9,8},{10,9},{11,10},{13,12},{... | collective-permute-start | bytes 196616 | tf_op jit(solution)/shard_map/ppermute | solution.py:10
  18.4 1.8 %copy-start = (f32[16,16,1024]{2,1,0:T(8,128)S(1)}, f32[16,16,1024]{2,1,0:T(8,128)}, u32[]{:S(2)}) copy-start(f32[16,16,1024]{2,1,0:T(8,128)} %param.7) | copy-start | bytes 3145732
Sparse Core Ops, SparseCore 0:
  82.9 69.5 all-reduce.2
where the time goes:
time: 161 us
  waiting for transfers between devices  74.8 us (46%)
  other arithmetic  33.3 us (21%)
  blocking collectives  32.2 us (20%)
  between operations  14.2 us (9%)
  local copies, waits for them, and re-layouts  3.52 us (2%)
  starting transfers between devices  2.75 us (2%)
    psum x1, waiting for transfers between devices, on_device(): radiance = lax.psum(front * light, 'depth')  69.7 us
    all_gather x1, blocking collectives, on_device(): pieces = lax.all_gather(depth_sum[None], 'depth', axis=0, tiled=True)  32.2 us
    another operation x1, other arithmetic, composite(): inclusive = jnp.cumsum(absorption, 0)  28.9 us
    ppermute x2, waiting for transfers between devices, from_behind(): return lax.ppermute(block, axis, route)  5.18 us
  transfers between devices with their start and end apart: 3, of which 3 were waited for; matrix products, arithmetic and copies ran while one was open for 1% of the time, Pallas kernels for 0%

commit v1 on v0

--- a/solution.py
+++ b/solution.py
@@ -60,7 +60,9 @@
     absorption = absorption * brick_mask[None, None, :]
     light, depth_sum = composite(absorption, emission)
     position = lax.axis_index("depth")
-    pieces = lax.all_gather(depth_sum[None], "depth", axis=0, tiled=True)
+    block_2 = depth_sum[None]
+    sent = jnp.stack([block_2] * lax.axis_size("depth"))
+    pieces = jnp.concatenate(lax.all_to_all(sent, "depth", 0, 0), axis=0)
     shard_ids = jnp.arange(pieces.shape[0], dtype=jnp.int32)
     in_front = (shard_ids < position)[:, None, None]
     front_depth = jnp.sum(jnp.where(in_front, pieces, 0.0), 0)

time: 161 us -> 151 us (0.938)
  blocking collectives: 32.2 us -> 0 us
  waiting for transfers between devices: 74.8 us -> 88.8 us
  starting transfers between devices: 2.75 us -> 8.82 us
    all_gather x1 -> x0, blocking collectives: 32.2 us -> none  [on_device(): pieces = lax.all_gather(depth_sum[None], 'depth', axis=0, tiled=True)]
    all_to_all x0 -> x1, waiting for transfers between devices: none -> 14.8 us  [on_device(): pieces = jnp.concatenate(lax.all_to_all(sent, 'depth', 0, 0), axis=0)]
    all_to_all x0 -> x1, starting transfers between devices: none -> 6.21 us  [on_device(): pieces = jnp.concatenate(lax.all_to_all(sent, 'depth', 0, 0), axis=0)]
  transfers between devices with their start and end apart: 3 -> 4, of which waited for: 3 -> 4; matrix products, arithmetic and copies ran while one was open for 1% -> 1% of each run, Pallas kernels for 0% -> 0%
where the time goes in v1:
time: 151 us; the launch traced here: 150 us
  waiting for transfers between devices  88.8 us (59%)
  other arithmetic  33.3 us (22%)
  between operations  14.2 us (9%)
  starting transfers between devices  8.82 us (6%)
  local copies, waits for them, and re-layouts  5.06 us (3%)
    psum x1, waiting for transfers between devices, on_device(): radiance = lax.psum(front * light, 'depth')  69.3 us
    another operation x1, other arithmetic, composite(): inclusive = jnp.cumsum(absorption, 0)  28.8 us
    all_to_all x1, waiting for transfers between devices, on_device(): pieces = jnp.concatenate(lax.all_to_all(sent, 'depth', 0, 0), axis=0)  14.8 us
    all_to_all x1, starting transfers between devices, on_device(): pieces = jnp.concatenate(lax.all_to_all(sent, 'depth', 0, 0), axis=0)  6.21 us
    ppermute x2, waiting for transfers between devices, from_behind(): return lax.ppermute(block, axis, route)  4.62 us
  transfers between devices with their start and end apart: 4, of which 4 were waited for; matrix products, arithmetic and copies ran while one was open for 1% of the time, Pallas kernels for 0%

profile of v1, /device:TPU:0, one launch (start us, length us, event | category | flops | bytes accessed | tf_op | source)
XLA Modules:
  0.0 150.2 jit_solution(3538832371163876174)
XLA Ops:
  7.2 0.0 copy-start.5
  7.2 0.0 copy-start.1
  7.2 0.9 slice.116
  8.0 1.3 collective-permute-start
  9.4 0.0 copy-start.6
  9.4 0.6 copy-done.6
  10.0 0.1 broadcast_bitcast_fusion
  10.1 0.6 copy-done.2
  10.7 0.0 copy-done.3
  10.7 0.0 copy-done.4
  10.7 0.1 select_reduce_fusion
  10.8 0.7 fusion.59
  11.5 3.6 %collective-permute-done = f32[1,16,1024]{2,1,0:T(8,128)S(1)} collective-permute-done((f32[1,16,1024]{2,1,0:T(8,128)S(1)}, f32[1,16,1024]{2,1,0:T(8,128)S(1)}, u32[]{:S(2)}, u32[]{:S(2)}) %collective-permute-start) | collective-permute-done | bytes 65568 | tf_op jit(solution)/shard_map/ppermute | solution.py:10
  15.1 1.7 %fusion.3 = f32[16,16,1024]{2,1,0:T(8,128)S(1)} fusion(f32[16,16,1024]{2,1,0:T(8,128)} %param.7, f32[1,16,1024]{2,1,0:T(8,128)S(1)} %collective-permute-done), kind=kLoop, calls=%fused_computation.24 | loop fusion | flops 786432 | bytes 2162688 | tf_op jit(solution)/shard_map/mul | solution.py:50
  16.9 1.3 collective-permute-start.1
  18.2 0.7 fusion.58
  19.0 0.0 copy-start
  19.0 0.1 slice.155
  19.1 1.0 collective-permute-done.1
  20.1 0.1 copy-done
  20.2 0.3 fusion.1
  20.5 0.3 slice.157
  20.9 28.8 %multiply_reduce_fusion = (f32[16,1024]{1,0:T(8,128)S(1)}, f32[16,16,1024]{2,1,0:T(8,128)S(1)}) fusion(f32[]{:T(128)} %bitcast.36, f32[]{:T(128)} %bitcast.35, f32[]{:T(128)} %bitcast.34, f32[]{:T(128)} %bitcast.33, f32[]{:T(128)} %bitcast.32, f32[]{:T(128)} %bitcast.31, f32[]{:T(128)} %bitcast.30, f32[]{:T(128)} %bitcast.29, f32[]{:T(128)} %bitcast.28, ...), kind=kOutput, calls=%fused_computation.4 | output fusion | flops 65781760 | bytes 3222656 | tf_op jit(solution)/shard_map/jit(cumsum)/reduce_window_sum | solution.py:41
  49.7 0.8 stack.10
  50.5 6.2 %all-to-all-start = ((f32[8,1,16,1024]{3,2,1,0:T(8,128)}), f32[8,1,16,1024]{3,2,1,0:T(8,128)S(1)}, u32[]{:S(2)}, u32[]{:S(2)}) async-start(f32[8,1,16,1024]{3,2,1,0:T(8,128)} %stack.10), calls=%async_computation | async-start | bytes 1048576 | tf_op jit(solution)/shard_map/all_to_all | solution.py:65
  56.7 0.0 all-reduce.3.cloned.1.call-start
  56.8 14.8 %all-to-all-done = f32[8,1,16,1024]{3,2,1,0:T(8,128)S(1)} async-done(((f32[8,1,16,1024]{3,2,1,0:T(8,128)}), f32[8,1,16,1024]{3,2,1,0:T(8,128)S(1)}, u32[]{:S(2)}, u32[]{:S(2)}) %all-to-all-start) | async-done | bytes 524320 | tf_op jit(solution)/shard_map/all_to_all | solution.py:65
  71.6 0.1 fusion.4
  71.8 0.7 multiply_bitcast_fusion
  72.4 0.0 all-reduce.3.cloned.1.call-update
  72.5 69.3 %all-reduce.3.cloned.1.call-done = f32[1,16,1024]{2,1,0:T(8,128)} async-done(((f32[1,16,1024]{2,1,0:T(8,128)}), f32[1,16,1024]{2,1,0:T(8,128)}) %all-reduce.3.cloned.1.call-update) | async-done | bytes 65552 | tf_op jit(solution)/shard_map/psum | solution.py:71
  141.8 1.5 %pad_maximum_fusion.1 = f32[2,16,1024]{2,1,0:T(8,128)} fusion(f32[1,16,1024]{2,1,0:T(8,128)S(1)} %exponential_bitcast_fusion, f32[1,16,1024]{2,1,0:T(8,128)} %all-reduce.3.cloned.1.call-done), kind=kLoop, calls=%fused_computation.61 | loop fusion | flops 32768 | bytes 262144 | tf_op jit(solution)/shard_map/stack | solution.py:72
  (13 shorter events, 0.1 us)
Async XLA Ops:
  7.2 2.2 %copy-start.5 = (s32[16]{0:T(128)S(1)}, s32[16]{0:T(128)}, u32[]{:S(2)}) copy-start(s32[16]{0:T(128)} %param.13) | copy-start | bytes 196
  7.2 2.2 %copy-start.1 = (s32[1024]{0:T(1024)S(1)}, s32[1024]{0:T(1024)}, u32[]{:S(2)}) copy-start(s32[1024]{0:T(1024)} %param.12) | copy-start | bytes 12292
  8.0 7.1 %collective-permute-start = (f32[1,16,1024]{2,1,0:T(8,128)S(1)}, f32[1,16,1024]{2,1,0:T(8,128)S(1)}, u32[]{:S(2)}, u32[]{:S(2)}) collective-permute-start(f32[1,16,1024]{2,1,0:T(8,128)S(1)} %slice.116), channel_id=1, source_target_pairs={{4,0},{8,4},{12,8},{16,12},{20,16},{24,20},{28,24},{5,1},{9,5},{13... | collective-permute-start | bytes 196616 | tf_op jit(solution)/shard_map/ppermute | solution.py:10
  9.4 0.7 copy-start.6
  10.0 0.7 copy-start.2
  10.0 0.7 copy-start.3
  10.0 0.7 copy-start.4
  16.9 3.1 %collective-permute-start.1 = (f32[16,1,1024]{2,1,0:T(1,128)S(1)}, f32[16,1,1024]{2,1,0:T(1,128)S(1)}, u32[]{:S(2)}, u32[]{:S(2)}) collective-permute-start(f32[16,1,1024]{2,1,0:T(1,128)S(1)} %slice.156), channel_id=1, source_target_pairs={{1,0},{2,1},{3,2},{5,4},{6,5},{7,6},{9,8},{10,9},{11,10},{13,12},{... | collective-permute-start | bytes 196616 | tf_op jit(solution)/shard_map/ppermute | solution.py:10
  19.0 1.2 copy-start
  50.5 21.1 %all-to-all-start = ((f32[8,1,16,1024]{3,2,1,0:T(8,128)}), f32[8,1,16,1024]{3,2,1,0:T(8,128)S(1)}, u32[]{:S(2)}, u32[]{:S(2)}) async-start(f32[8,1,16,1024]{3,2,1,0:T(8,128)} %stack.10), calls=%async_computation | async-start | bytes 1048576 | tf_op jit(solution)/shard_map/all_to_all | solution.py:65
  56.7 85.1 %all-reduce.3.cloned.1.call-start = ((), (), s32[]{:S(2)}) async-start(), calls=%async_computation.1 | async-start | bytes 131072 | tf_op jit(solution)/shard_map/psum | solution.py:71
Sparse Core Ops, SparseCore 0:
  72.6 69.2 all-reduce.2
